TPU v7x, 32 devices: a whole 2x2x4 slice. The times are simulated.
32 devices in a mesh: mp: 8 (over z, x), dp: 4 (over y, core).
Axes of the slice: x: 2, y: 2, z: 4, core: 2. Of those that a mesh axis runs over, the one named last changes fastest.
Arguments:
- tables: bfloat16 [20, 16384, 128], P(None, 'mp'), may hold values from -3 to 3
- block_rows: int32 [2048, 128], P(('mp', 'dp')), may hold values from 0 to 2047
- block_slots: int32 [2048, 128], P(('mp', 'dp')), may hold values from 0 to 127
- block_table: int32 [2048], P(('mp', 'dp')), may hold values from 0 to 19
- block_peer: int32 [2048, 1], P(('mp', 'dp')), may hold values from 0 to 7; in each aligned block of 64 rows (0 to 63, 64 to 127, ...) at most 16 rows name the same one
- block_len: int32 [2048], P(('mp', 'dp')), may hold values from 1 to 128
- block_count: int32 [32], P(('mp', 'dp')), may hold values from 1 to 64, as said below
- cross_in: bfloat16 [4, 2560, 256], P(None, 'dp'), may hold values from -0.23632812 to 0.23632812
- cross_mix: bfloat16 [4, 256, 256], replicated, may hold values from -0.5625 to 0.5625
- cross_out: bfloat16 [4, 256, 2560], P(None, None, 'dp'), may hold values from -0.375 to 0.375
- cross_bias: float32 [4, 2560], replicated, may hold values from -3 to 3
- gate_weight: bfloat16 [4, 2560], replicated, may hold values from -0.47265625 to 0.47265625
Outputs:
- crossed: bfloat16 [4096, 2560], P(('mp', 'dp'))
Inputs may be any that keep to these rules, and one draw needn't show every extreme that they name: `block_peer`: in the 64 blocks of one device no destination is named by more than 16 blocks, a bound that the blocks of some device reach. The live blocks of a device are its first block_count blocks; some device has exactly 64. Entries of a block at positions below its block_len are live. `block_rows`: A row index within the device's own shard of the table. `block_slots`: A sample of the destination device.
All inputs are finite; a program needn't handle non-finite values.
Results may differ from a plain program's by a relative error of at most 0.0059.
Values may be sent and summed in bfloat16 or wider, within the bound.
A program may use at most 128 MiB of HBM per device.

v0:
```python
import jax
import jax.numpy as jnp
from jax import lax
from jax.sharding import PartitionSpec as P

B_DEV = 128


blocks_per_turn = 8


def pick_rows(tables, block_rows, block_table, first):
    row_ids = lax.dynamic_slice_in_dim(block_rows, first, blocks_per_turn, 0)
    table_ids = lax.dynamic_slice_in_dim(block_table, first, blocks_per_turn, 0)
    return tables[table_ids[:, None], row_ids]


def on_device(
    tables,
    block_rows,
    block_slots,
    block_table,
    block_peer,
    block_len,
    block_count,
    cross_in,
    cross_mix,
    cross_out,
    cross_bias,
    gate_weight,
):
    peers = lax.axis_size("mp")
    total_blocks, block_width = block_rows.shape
    table_count, rows_dev, width = tables.shape
    samples = B_DEV
    count = block_count[0]
    turns = (count + blocks_per_turn - 1) // blocks_per_turn
    peer_ids = block_peer[:, 0]
    entries = jnp.arange(block_width, dtype=jnp.int32)
    sample_ids = jnp.arange(samples, dtype=jnp.int32)
    capacity = max(2, 2 * total_blocks // peers)

    def gather_turn(turn, store):
        first = turn * blocks_per_turn
        picked = pick_rows(tables, block_rows, block_table, first)
        return lax.dynamic_update_slice_in_dim(store, picked, first, 0)

    stored = lax.fori_loop(
        0, turns, gather_turn, jnp.zeros((total_blocks, block_width, width), jnp.bfloat16)
    )
    live_block = jnp.arange(total_blocks, dtype=jnp.int32) < count
    peer_table = (
        (peer_ids[:, None] == jnp.arange(peers, dtype=jnp.int32)[None, :]) & live_block[:, None]
    ).astype(jnp.int32)
    before = jnp.cumsum(peer_table, axis=0) - peer_table
    position = jnp.sum(before * peer_table, axis=1)
    target = jnp.where(live_block, peer_ids * capacity + position, peers * capacity)
    live_entry = (entries[None, :] < block_len[:, None]) & live_block[:, None]
    code = jnp.where(live_entry, block_table[:, None] * samples + block_slots, -1)
    send_rows = (
        jnp.zeros((peers * capacity, block_width, width), jnp.bfloat16)
        .at[target]
        .set(stored, mode="drop")
    )
    send_code = (
        jnp.full((peers * capacity, block_width), -1, jnp.int32).at[target].set(code, mode="drop")
    )
    arrived_rows, arrived_code = (
        lax.all_to_all(
            send_rows.reshape(peers, capacity, block_width, width),
            "mp",
            split_axis=0,
            concat_axis=0,
            tiled=True,
        ),
        lax.all_to_all(
            send_code.reshape(peers, capacity, block_width),
            "mp",
            split_axis=0,
            concat_axis=0,
            tiled=True,
        ),
    )
    flat_rows = arrived_rows.reshape(peers * capacity, block_width, width)
    flat_code = arrived_code.reshape(peers * capacity, block_width)
    slot_of = jnp.where(flat_code >= 0, flat_code % samples, -1)
    onehot = (slot_of[:, :, None] == sample_ids[None, None, :]).astype(jnp.bfloat16)
    contrib = jnp.einsum("kis,kiw->ksw", onehot, flat_rows, preferred_element_type=jnp.float32)
    top_code = jnp.max(flat_code, axis=1)
    slot_live = top_code >= 0
    table_of = jnp.maximum(top_code, 0) // samples
    table_grid = table_of.reshape(peers, capacity)
    live_grid = slot_live.reshape(peers, capacity)
    same = (
        (table_grid[:, :, None] == table_grid[:, None, :])
        & live_grid[:, :, None]
        & live_grid[:, None, :]
    )
    grouped = jnp.einsum(
        "pkj,pjx->pkx",
        same.astype(jnp.float32),
        contrib.reshape(peers, capacity, samples * width),
        precision=lax.Precision.HIGHEST,
    )
    rounded = grouped.astype(jnp.bfloat16).astype(jnp.float32)
    slot_order = jnp.arange(capacity, dtype=jnp.int32)
    earlier = jnp.sum(same & (slot_order[None, None, :] < slot_order[None, :, None]), axis=2)
    leader = (live_grid & (earlier == 0)).reshape(peers * capacity)
    owner = (
        (table_of[:, None] == jnp.arange(table_count, dtype=jnp.int32)[None, :]) & leader[:, None]
    ).astype(jnp.float32)
    summed = jnp.einsum(
        "kt,kx->tx",
        owner,
        rounded.reshape(peers * capacity, samples * width),
        precision=lax.Precision.HIGHEST,
    )
    embedded = (
        summed.reshape(table_count, samples, width)
        .transpose(1, 0, 2)
        .reshape(samples, table_count * width)
        .astype(jnp.bfloat16)
    )
    gate = jax.nn.sigmoid(jnp.dot(embedded, gate_weight.T, preferred_element_type=jnp.float32))
    projected = jnp.einsum(
        "bn,enr->ebr",
        embedded,
        lax.all_gather(cross_in, "dp", axis=1, tiled=True),
        preferred_element_type=jnp.float32,
    )
    hidden = jnp.tanh(projected).astype(jnp.bfloat16)
    mixed = jnp.tanh(
        jnp.einsum("ebr,erq->ebq", hidden, cross_mix, preferred_element_type=jnp.float32)
    ).astype(jnp.bfloat16)
    gate_columns = gate.T
    grown = jnp.einsum(
        "ebr,ern->ebn",
        mixed,
        lax.all_gather(cross_out, "dp", axis=2, tiled=True),
        preferred_element_type=jnp.float32,
    )
    grown = grown + cross_bias[:, None, :]
    weighted = jnp.sum(gate_columns[:, :, None] * grown, axis=0)
    base = embedded.astype(jnp.float32)
    return (base + base * weighted).astype(jnp.bfloat16)


def solution(mesh):
    in_specs = (
        P(None, "mp", None),
        P(("mp", "dp"), None),
        P(("mp", "dp"), None),
        P(("mp", "dp")),
        P(("mp", "dp"), None),
        P(("mp", "dp")),
        P(("mp", "dp")),
        P(None, "dp", None),
        P(),
        P(None, None, "dp"),
        P(),
        P(),
    )
    out_specs = P(("mp", "dp"), None)
    return jax.shard_map(
        on_device, mesh=mesh, in_specs=in_specs, out_specs=out_specs, check_vma=False
    )
```

profile of v0, /device:TPU:1, one launch (start us, length us, event | category | flops | bytes accessed | tf_op | source)
XLA Modules:
  0.0 275.8 jit_solution(15117308623539063028)
XLA Ops:
  6.5 0.7 all-gather.3.cloned.1.call-update
  7.9 0.7 fusion.28
  8.8 0.8 select_reduce_fusion
  9.6 0.7 broadcast_multiply_fusion
  10.3 0.7 fusion.43
  10.9 1.6 scatter_custom_fusion
  12.6 6.3 %all-to-all-start = ((s32[8,16,128]{2,1,0:T(8,128)}), s32[8,16,128]{2,1,0:T(8,128)S(1)}, u32[]{:S(2)}, u32[]{:S(2)}) async-start(s32[8,16,128]{2,1,0:T(8,128)} %bitcast.7), calls=%async_computation | async-start | bytes 131072 | tf_op jit(solution)/shard_map/all_to_all | solution.py:76
  19.4 58.9 %while.10 = (s32[]{:T(128)}, bf16[64,128,128]{2,1,0:T(8,128)(2,1)S(1)}, s32[]{:T(128)}, s32[64]{0:T(128)}, s32[64,128]{1,0:T(8,128)}, /*index=5*/bf16[20,2048,12...) while((s32[]{:T(128)}, bf16[64,128,128]{2,1,0:T(8,128)(2,1)S(1)}, s32[]{:T(128)}, ...), condition=%wide.region_6.7_spmd, body=%wide.region_5.6_spmd.sunk | while | flops 6190 | bytes 1065215 | solution.py:48
  19.4 0.7 fusion.57
  20.2 0.8 fusion.58
  21.0 13.1 %gather_fusion = bf16[1024,128]{1,0:T(8,128)(2,1)S(1)} fusion(bf16[20,2048,128]{2,1,0:T(8,128)(2,1)} %get-tuple-element.117, s32[1024]{0:T(1024)S(1)} %fusion.58), kind=kCustom, calls=%fused_computation.clone.1 | custom fusion | bytes 532480 | tf_op jit(solution)/shard_map/while/body/gather | solution.py:15
  34.1 0.7 fusion.57
  34.9 0.8 fusion.58
  35.6 13.1 %gather_fusion = bf16[1024,128]{1,0:T(8,128)(2,1)S(1)} fusion(bf16[20,2048,128]{2,1,0:T(8,128)(2,1)} %get-tuple-element.117, s32[1024]{0:T(1024)S(1)} %fusion.58), kind=kCustom, calls=%fused_computation.clone.1 | custom fusion | bytes 532480 | tf_op jit(solution)/shard_map/while/body/gather | solution.py:15
  48.8 0.7 fusion.57
  49.6 0.8 fusion.58
  50.3 13.2 %gather_fusion = bf16[1024,128]{1,0:T(8,128)(2,1)S(1)} fusion(bf16[20,2048,128]{2,1,0:T(8,128)(2,1)} %get-tuple-element.117, s32[1024]{0:T(1024)S(1)} %fusion.58), kind=kCustom, calls=%fused_computation.clone.1 | custom fusion | bytes 532480 | tf_op jit(solution)/shard_map/while/body/gather | solution.py:15
  63.6 0.7 fusion.57
  64.3 0.8 fusion.58
  65.1 13.2 %gather_fusion = bf16[1024,128]{1,0:T(8,128)(2,1)S(1)} fusion(bf16[20,2048,128]{2,1,0:T(8,128)(2,1)} %get-tuple-element.117, s32[1024]{0:T(1024)S(1)} %fusion.58), kind=kCustom, calls=%fused_computation.clone.1 | custom fusion | bytes 532480 | tf_op jit(solution)/shard_map/while/body/gather | solution.py:15
  78.4 3.0 %broadcast_in_dim.28 = bf16[128,128,128]{2,1,0:T(8,128)(2,1)} broadcast(bf16[]{:T(256)} %constant.83.clone.1), dimensions={} | broadcast | bytes 4194306 | tf_op jit(solution)/shard_map/broadcast_in_dim | solution.py:61
  81.4 8.0 %scatter_fusion = bf16[128,128,128]{2,1,0:T(8,128)(2,1)} fusion(bf16[128,128,128]{2,1,0:T(8,128)(2,1)} %broadcast_in_dim.28, s32[64]{0:T(128)S(1)} %fusion.43, bf16[64,128,128]{2,1,0:T(8,128)(2,1)S(1)} %get-tuple-element.38), kind=kCustom, calls=%fused_computation.2 | custom fusion | bytes 6291712 | tf_op jit(solution)/shard_map/scatter | solution.py:63
  89.4 50.4 %all-to-all-start.1 = ((bf16[8,16,128,128]{3,2,1,0:T(8,128)(2,1)}), bf16[8,16,128,128]{3,2,1,0:T(8,128)(2,1)}, u32[]{:S(2)}, u32[]{:S(2)}) async-start(bf16[8,16,128,128]{3,2,1,0:T(8,128)(2,1)} %bitcast.70), calls=%async_computation.1 | async-start | bytes 8388608 | tf_op jit(solution)/shard_map/all_to_all | solution.py:69
  141.4 82.9 %all-to-all-done.1 = bf16[8,16,128,128]{3,2,1,0:T(8,128)(2,1)} async-done(((bf16[8,16,128,128]{3,2,1,0:T(8,128)(2,1)}), bf16[8,16,128,128]{3,2,1,0:T(8,128)(2,1)}, u32[]{:S(2)}, u32[]{:S(2)}) %all-to-all-start.1) | async-done | bytes 4194336 | tf_op jit(solution)/shard_map/all_to_all | solution.py:69
  224.3 6.7 %fusion.7 = f32[128,128,128]{2,1,0:T(8,128)} fusion(bf16[128,128,128]{2,1,0:T(8,128)(2,1)} %bitcast.11, s32[128,128]{1,0:T(8,128)S(1)} %fusion.19), kind=kOutput, calls=%fused_computation.15 | convolution fusion | flops 538968064 | bytes 12648448 | tf_op jit(solution)/shard_map/kis,kiw->ksw/dot_general | solution.py:88
  231.0 9.4 %reshape.165 = f32[8,16,16384]{2,1,0:T(8,128)} reshape(f32[128,128,128]{2,1,0:T(8,128)} %fusion.7) | data formatting | bytes 16777216 | tf_op jit(solution)/shard_map/reshape | solution.py:102
  240.4 9.6 %convolution_convert_fusion = bf16[8,16,16384]{2,1,0:T(8,128)(2,1)} fusion(f32[8,16,16384]{2,1,0:T(8,128)} %reshape.165, s32[8,16]{1,0:T(8,128)S(1)} %get-tuple-element.51, pred[8,16]{1,0:T(8,128)(4,1)S(1)} %broadcast_compare_fusion), kind=kOutput, calls=%fused_computation.13 | convolution fusion | flops 404756480 | bytes 12583552 | tf_op jit(solution)/shard_map/pkj,pjx->pkx/dot_general | solution.py:99
  249.9 6.4 %copy.17 = bf16[16384,128]{1,0:T(8,128)(2,1)} copy(bf16[16384,128]{0,1:T(8,128)(2,1)} %bitcast.72) | data formatting | bytes 8388608 | tf_op jit(solution)/shard_map/kt,kx->tx/dot_general | solution.py:112
  256.3 3.4 %fusion.10 = bf16[128,20,128]{2,1,0:T(8,128)(2,1)S(1)} fusion(bf16[128,128,128]{2,1,0:T(8,128)(2,1)} %bitcast.73, s32[128]{0:T(128)S(1)} %add_select_fusion.2, pred[128]{0:T(512)(128)(4,1)S(1)} %and.121), kind=kOutput, calls=%fused_computation.21 | convolution fusion | flops 84218880 | bytes 4850304 | tf_op jit(solution)/shard_map/kt,kx->tx/dot_general | solution.py:112
  260.7 3.5 %fusion.12 = bf16[4,128,256]{2,1,0:T(8,128)(2,1)S(1)} fusion(bf16[4,256,256]{2,1,0:T(8,128)(2,1)S(1)} %copy-done, bf16[128,2560,1]{0,1,2:T(8,128)(2,1)S(1)} %bitcast.76, bf16[4,2560,256]{2,1,0:T(8,128)(2,1)} %all-gather.3.cloned.1.call-done), kind=kOutput, calls=%fused_computation.25 | convolution fusion | flops 738459648 | bytes 6684672 | tf_op jit(solution)/shard_map/ebr,erq->ebq/dot_general | solution.py:133
  264.3 3.6 %multiply_reduce_fusion = f32[128,2560]{1,0:T(8,128)S(1)} fusion(bf16[4,128,256]{2,1,0:T(8,128)(2,1)S(1)} %fusion.12, bf16[4,256,2560]{2,1,0:T(8,128)(2,1)} %all-gather.5.cloned.1.call-done, f32[4,2560]{1,0:T(4,128)S(1)} %copy-done.2, f32[4,128]{1,0:T(4,128)S(1)} %fusion.17), kind=kOutput, calls=%fused_computation.16 | convolution fusion | flops 674693120 | bytes 6858752 | tf_op jit(solution)/shard_map/ebr,ern->ebn/dot_general | solution.py:136
  267.9 1.0 fusion.9
  (33 shorter events, 3.3 us)
Async XLA Ops:
  6.5 254.2 %copy-start = (bf16[4,256,256]{2,1,0:T(8,128)(2,1)S(1)}, bf16[4,256,256]{2,1,0:T(8,128)(2,1)}, u32[]{:S(2)}) copy-start(bf16[4,256,256]{2,1,0:T(8,128)(2,1)} %param.22) | copy-start | bytes 1572868
  6.5 254.1 %all-gather.3.cloned.1.call-start = ((), (), s32[]{:S(2)}) async-start(), calls=%async_computation.2 | async-start | bytes 6553600 | tf_op jit(solution)/shard_map/all_gather | solution.py:128
  12.6 76.9 %all-to-all-start = ((s32[8,16,128]{2,1,0:T(8,128)}), s32[8,16,128]{2,1,0:T(8,128)S(1)}, u32[]{:S(2)}, u32[]{:S(2)}) async-start(s32[8,16,128]{2,1,0:T(8,128)} %bitcast.7), calls=%async_computation | async-start | bytes 131072 | tf_op jit(solution)/shard_map/all_to_all | solution.py:76
  89.4 134.9 %all-to-all-start.1 = ((bf16[8,16,128,128]{3,2,1,0:T(8,128)(2,1)}), bf16[8,16,128,128]{3,2,1,0:T(8,128)(2,1)}, u32[]{:S(2)}, u32[]{:S(2)}) async-start(bf16[8,16,128,128]{3,2,1,0:T(8,128)(2,1)} %bitcast.70), calls=%async_computation.1 | async-start | bytes 8388608 | tf_op jit(solution)/shard_map/all_to_all | solution.py:69
  139.8 124.4 %all-gather.5.cloned.1.call-start = ((), (), s32[]{:S(2)}) async-start(), calls=%async_computation.3 | async-start | bytes 6553600 | tf_op jit(solution)/shard_map/all_gather | solution.py:139
  256.3 4.2 %copy-start.1 = (bf16[4,2560]{1,0:T(4,128)(2,1)S(1)}, bf16[4,2560]{1,0:T(4,128)(2,1)}, u32[]{:S(2)}) copy-start(bf16[4,2560]{1,0:T(4,128)(2,1)} %param.25) | copy-start | bytes 61444
  260.2 4.1 %copy-start.2 = (f32[4,2560]{1,0:T(4,128)S(1)}, f32[4,2560]{1,0:T(4,128)}, u32[]{:S(2)}) copy-start(f32[4,2560]{1,0:T(4,128)} %param.24) | copy-start | bytes 122884
Sparse Core Ops, SparseCore 0:
  8.9 42.9 all-gather.2
  142.2 55.2 all-gather.4
where the time goes:
time: 273 us; the launch traced here: 276 us
  waiting for transfers between devices  84.1 us (31%)
  local copies, waits for them, and re-layouts  81.1 us (30%)
  starting transfers between devices  57 us (21%)
  matrix products  27 us (10%)
  between operations  14.2 us (5%)
  other arithmetic  12.2 us (4%)
    all_to_all x1, waiting for transfers between devices, on_device(): lax.all_to_all(send_rows.reshape(peers, capacity, block_width, width), 'm...  82.9 us
    gather x4, local copies, waits for them, and re-layouts, pick_rows(): return tables[table_ids[:, None], row_ids]  52.6 us
    all_to_all x1, starting transfers between devices, on_device(): lax.all_to_all(send_rows.reshape(peers, capacity, block_width, width), 'm...  50.4 us
    dot_general x1, matrix products, on_device(): jnp.einsum('pkj,pjx->pkx', same.astype(jnp.float32), contrib.reshape(peer...  9.57 us
    reshape x1, local copies, waits for them, and re-layouts, on_device(): contrib.reshape(peers, capacity, samples * width)  9.39 us
    scatter x1, local copies, waits for them, and re-layouts, on_device(): send_rows = jnp.zeros((peers * capacity, block_width, width), jnp.bfloat1...  8.05 us
    dot_general x1, matrix products, on_device(): jnp.einsum('kis,kiw->ksw', onehot, flat_rows, preferred_element_type=jnp....  6.65 us
    dot_general x1, local copies, waits for them, and re-layouts, on_device(): jnp.einsum('kt,kx->tx', owner, rounded.reshape(peers * capacity, samples...  6.37 us
  transfers between devices with their start and end apart: 4, of which 1 were waited for; matrix products, arithmetic and copies ran while one was open for 42% of the time, Pallas kernels for 0%

commit v1 on v0

v1 whole, which is shorter than its diff:
```python
import functools

import jax
import jax.numpy as jnp
from jax import lax
from jax.experimental import pallas as pl
from jax.experimental.pallas import tpu as pltpu
from jax.sharding import PartitionSpec as P

B_DEV = 128
UNROLL = 4
STREAMS = 4
MESH = pl.DeviceIdType.MESH
VMEM_LIMIT = 67043328


def pool_kernel(
    unroll,
    count_ref,
    table_ref,
    peer_ref,
    len_ref,
    rows_ref,
    slots_ref,
    tables_ref,
    out_ref,
    acc,
    slot_of,
    key_of,
):
    table_count, rows_dev, width = tables_ref.shape
    total_blocks, block = rows_ref.shape
    tiles, samples, _ = out_ref.shape
    count = count_ref[0]

    def clear(i, carry):
        out_ref[i] = jnp.zeros((samples, width), jnp.bfloat16)
        slot_of[i] = -1
        return carry

    lax.fori_loop(0, tiles, clear, 0)

    lane = lax.broadcasted_iota(jnp.int32, (block, 128), 1)
    sample = lax.broadcasted_iota(jnp.int32, (samples, block), 0)
    entry = lax.broadcasted_iota(jnp.int32, (samples, block), 1)

    def group(g, used):
        made = []
        for u in range(unroll):
            b = g * unroll + u
            row = rows_ref[pl.ds(b, 1), :]
            slot = slots_ref[pl.ds(b, 1), :]
            table = table_ref[b]
            column = jnp.broadcast_to(row, (128, block)).T
            pick = jnp.concatenate(
                [
                    jnp.where(column == lane + c * 128, 1.0, 0.0).astype(jnp.bfloat16)
                    for c in range(rows_dev // 128)
                ],
                axis=1,
            )
            picked = jnp.dot(pick, tables_ref[table], preferred_element_type=jnp.float32)
            place = jnp.where((sample == slot) & (entry < len_ref[b]), 1.0, 0.0)
            made.append(
                jnp.dot(
                    place.astype(jnp.bfloat16),
                    picked.astype(jnp.bfloat16),
                    preferred_element_type=jnp.float32,
                )
            )
        for u in range(unroll):
            b = g * unroll + u
            key = peer_ref[b] * table_count + table_ref[b]
            live = b < count
            known = slot_of[key]
            first = known < 0
            at = jnp.where(live, jnp.where(first, used, known), total_blocks)
            acc[at] = jnp.where(first, made[u], acc[at] + made[u])
            slot_of[key] = jnp.where(live, at, known)
            key_of[at] = key
            used = used + jnp.where(live & first, 1, 0)
        return used

    used = lax.fori_loop(0, (count + unroll - 1) // unroll, group, 0)

    def flush(i, carry):
        out_ref[key_of[i]] = acc[i].astype(jnp.bfloat16)
        return carry

    lax.fori_loop(0, used, flush, 0)


def pool(peers, tables, block_rows, block_slots, block_table, block_peer, block_len, block_count):
    table_count, _, width = tables.shape
    total_blocks = block_rows.shape[0]
    tiles = peers * table_count
    unroll = UNROLL if total_blocks % UNROLL == 0 else 1
    smem = pl.BlockSpec(memory_space=pltpu.SMEM)
    vmem = pl.BlockSpec(memory_space=pltpu.VMEM)
    return pl.pallas_call(
        functools.partial(pool_kernel, unroll),
        out_shape=jax.ShapeDtypeStruct((tiles, B_DEV, width), jnp.bfloat16),
        in_specs=[smem] * 4 + [vmem] * 3,
        out_specs=vmem,
        scratch_shapes=[
            pltpu.VMEM((total_blocks + 1, B_DEV, width), jnp.float32),
            pltpu.SMEM((tiles,), jnp.int32),
            pltpu.SMEM((total_blocks + 1,), jnp.int32),
        ],
        compiler_params=pltpu.CompilerParams(vmem_limit_bytes=VMEM_LIMIT),
        name="pool",
    )(block_count, block_table, block_peer[:, 0], block_len, block_rows, block_slots, tables)


def cross_kernel(
    peers,
    share,
    partial_ref,
    in_ref,
    mix_ref,
    out_w_ref,
    bias_ref,
    gate_ref,
    result_ref,
    held,
    emb,
    win,
    wout,
    ring_send,
    ring_recv,
    w_send,
    w_recv,
    w_local,
):
    tiles, samples, width = partial_ref.shape
    table_count = tiles // peers
    part = table_count // STREAMS
    experts = mix_ref.shape[0]
    me = lax.axis_index("mp")
    half = peers // 2
    at = jnp.where(lax.rem(me, 2) == 0, lax.div(me, 2), peers - 1 - lax.div(me, 2))

    def member(position):
        position = lax.rem(position + 2 * peers, peers)
        return jnp.where(position < half, 2 * position, 2 * (peers - 1 - position) + 1)

    ahead, behind = member(at + 1), member(at - 1)

    barrier = pltpu.get_barrier_semaphore()
    greet = [{"mp": ahead}, {"mp": behind}]
    if share:
        d = lax.axis_index("dp")
        twin = d + 1 - 2 * lax.rem(d, 2)
        across = lax.rem(d + 2, 4)
        greet += [{"dp": twin}, {"dp": across}]
    for target in greet:
        pl.semaphore_signal(barrier, inc=1, device_id=target, device_id_type=MESH)
    pl.semaphore_wait(barrier, len(greet))

    def ring_copy(stream, source, step):
        target = ahead if stream % 2 == 0 else behind
        return pltpu.make_async_remote_copy(
            src_ref=source,
            dst_ref=held.at[step, stream],
            send_sem=ring_send.at[stream, step],
            recv_sem=ring_recv.at[stream, step],
            device_id={"mp": target},
            device_id_type=MESH,
        )

    def own_tiles(stream, distance):
        dest = member(at - distance if stream % 2 == 0 else at + distance)
        return pl.ds(dest * table_count + stream * part, part)

    for stream in range(STREAMS):
        ring_copy(stream, partial_ref.at[own_tiles(stream, 1)], 0).start()

    if share:

        def piece_refs(q, owner):
            if q < experts:
                return in_ref.at[q], win.at[owner, q]
            return out_w_ref.at[q - experts], wout.at[owner, q - experts]

        def w_copy(kind, q):
            if kind == 0:
                source, place = piece_refs(q, d)
                target = across
            elif kind == 1:
                source, place = piece_refs(q, d)
                target = twin
            else:
                _, place = piece_refs(q, across)
                source = place
                target = twin
            return pltpu.make_async_remote_copy(
                src_ref=source,
                dst_ref=place,
                send_sem=w_send.at[kind, q],
                recv_sem=w_recv.at[kind, q],
                device_id={"dp": target},
                device_id_type=MESH,
            )

        pieces = 2 * experts
        for kind in (0, 1):
            for q in range(pieces):
                w_copy(kind, q).start()
        local = []
        for q in range(pieces):
            source, place = piece_refs(q, d)
            local.append(pltpu.make_async_copy(source, place, w_local.at[q]))
            local[-1].start()

    def hop(step, last):
        for stream in range(STREAMS):
            ring_copy(stream, held.at[step, stream], step).wait_recv()
            mine = partial_ref[own_tiles(stream, step + 2)]
            total = held[step, stream].astype(jnp.float32) + mine.astype(jnp.float32)
            total = total.astype(jnp.bfloat16)
            if last:
                for i in range(part):
                    column = (stream * part + i) * width
                    emb[:, column : column + width] = total[i]
            else:
                held[step, stream] = total
                ring_copy(stream, held.at[step, stream], step + 1).start()

    if share:
        passed = 0
        for step in range(peers - 2):
            hop(step, False)
            if 1 <= step and passed < pieces:
                w_copy(0, passed).wait_recv()
                w_copy(2, passed).start()
                passed += 1
        hop(peers - 2, True)
        for q in range(passed, pieces):
            w_copy(0, q).wait_recv()
            w_copy(2, q).start()
        for q in range(pieces):
            local[q].wait()
    else:

        def turn(step, carry):
            hop(step, False)
            return carry

        lax.fori_loop(0, peers - 2, turn, 0)
        hop(peers - 2, True)

    owners = win.shape[0] if share else 1
    depth = in_ref.shape[1]
    columns = out_w_ref.shape[2]
    gate = jax.nn.sigmoid(
        lax.dot_general(
            emb[...], gate_ref[...], (((1,), (1,)), ((), ())), preferred_element_type=jnp.float32
        )
    )
    mixed = []
    for e in range(experts):
        if share:
            w_copy(1, e).wait_recv()
            w_copy(2, e).wait_recv()
        projected = jnp.zeros((samples, in_ref.shape[2]), jnp.float32)
        for o in range(owners):
            weight = win[o, e] if share else in_ref[e]
            projected += jnp.dot(
                emb[:, o * depth : (o + 1) * depth], weight, preferred_element_type=jnp.float32
            )
        hidden = jnp.tanh(projected).astype(jnp.bfloat16)
        mixed.append(
            jnp.tanh(
                jnp.dot(hidden, mix_ref[e], preferred_element_type=jnp.float32)
            ).astype(jnp.bfloat16)
        )
    if share:
        for e in range(experts):
            w_copy(1, experts + e).wait_recv()
            w_copy(2, experts + e).wait_recv()
    for o in range(owners):
        span = slice(o * columns, (o + 1) * columns)
        weighted = jnp.zeros((samples, columns), jnp.float32)
        for e in range(experts):
            weight = wout[o, e] if share else out_w_ref[e]
            grown = jnp.dot(mixed[e], weight, preferred_element_type=jnp.float32)
            weighted += gate[:, e : e + 1] * (grown + bias_ref[e : e + 1, span])
        base = emb[:, span].astype(jnp.float32)
        result_ref[:, span] = (base + base * weighted).astype(jnp.bfloat16)

    for stream in range(STREAMS):
        ring_copy(stream, partial_ref.at[own_tiles(stream, 1)], 0).wait_send()

    def sent(step, carry):
        for stream in range(STREAMS):
            ring_copy(stream, held.at[step - 1, stream], step).wait_send()
        return carry

    lax.fori_loop(1, peers - 1, sent, 0)
    if share:
        for kind in (0, 1, 2):
            for q in range(pieces):
                w_copy(kind, q).wait_send()


def cross(peers, groups, partial, cross_in, cross_mix, cross_out, cross_bias, gate_weight):
    tiles, samples, width = partial.shape
    table_count = tiles // peers
    experts = cross_in.shape[0]
    share = groups == 4 and cross_out.shape[2] % 128 == 0 and peers <= 8
    if not share:
        cross_in = lax.all_gather(cross_in, "dp", axis=1, tiled=True)
        cross_out = lax.all_gather(cross_out, "dp", axis=2, tiled=True)
        kept = (1, 8, 128), (1, 8, 128)
    else:
        kept = (groups, *cross_in.shape), (groups, *cross_out.shape)
    vmem = pl.BlockSpec(memory_space=pltpu.VMEM)
    return pl.pallas_call(
        functools.partial(cross_kernel, peers, share),
        out_shape=jax.ShapeDtypeStruct((samples, table_count * width), jnp.bfloat16),
        in_specs=[vmem] * 6,
        out_specs=vmem,
        scratch_shapes=[
            pltpu.VMEM((peers - 1, STREAMS, table_count // STREAMS, samples, width), jnp.bfloat16),
            pltpu.VMEM((samples, table_count * width), jnp.bfloat16),
            pltpu.VMEM(kept[0], jnp.bfloat16),
            pltpu.VMEM(kept[1], jnp.bfloat16),
            pltpu.SemaphoreType.DMA((STREAMS, peers - 1)),
            pltpu.SemaphoreType.DMA((STREAMS, peers - 1)),
            pltpu.SemaphoreType.DMA((3, 2 * experts)),
            pltpu.SemaphoreType.DMA((3, 2 * experts)),
            pltpu.SemaphoreType.DMA((2 * experts,)),
        ],
        compiler_params=pltpu.CompilerParams(
            collective_id=0, has_side_effects=True, vmem_limit_bytes=VMEM_LIMIT
        ),
        name="cross",
    )(partial, cross_in, cross_mix, cross_out, cross_bias, gate_weight)


def on_device(
    tables,
    block_rows,
    block_slots,
    block_table,
    block_peer,
    block_len,
    block_count,
    cross_in,
    cross_mix,
    cross_out,
    cross_bias,
    gate_weight,
):
    peers, groups = lax.axis_size("mp"), lax.axis_size("dp")
    partial = pool(
        peers, tables, block_rows, block_slots, block_table, block_peer, block_len, block_count
    )
    return cross(peers, groups, partial, cross_in, cross_mix, cross_out, cross_bias, gate_weight)


def solution(mesh):
    in_specs = (
        P(None, "mp", None),
        P(("mp", "dp"), None),
        P(("mp", "dp"), None),
        P(("mp", "dp")),
        P(("mp", "dp"), None),
        P(("mp", "dp")),
        P(("mp", "dp")),
        P(None, "dp", None),
        P(),
        P(None, None, "dp"),
        P(),
        P(),
    )
    out_specs = P(("mp", "dp"), None)
    return jax.shard_map(
        on_device, mesh=mesh, in_specs=in_specs, out_specs=out_specs, check_vma=False
    )
```

time: 273 us -> 101 us (0.37)
  the two profiles are of different devices: /device:TPU:1 before, /device:TPU:25 now
where the time goes in v1:
time: 101 us
  Pallas kernels  97.9 us (97%)
  local copies, waits for them, and re-layouts  1.97 us (2%)
    pallas_call x1, Pallas kernels, cross(): pl.pallas_call(functools.partial(cross_kernel, peers, share), out_shape=j...  76.9 us
    pallas_call x1, Pallas kernels, pool(): pl.pallas_call(functools.partial(pool_kernel, unroll), out_shape=jax.Shap...  21 us

profile of v1, /device:TPU:25, one launch (start us, length us, event | category | flops | bytes accessed | tf_op | source)
XLA Modules:
  0.0 100.5 jit_solution(17687926334032732313)
XLA Ops:
  0.7 21.0 %pool.1.partial_ref = bf16[160,128,128]{2,1,0:T(8,128)(2,1)} custom-call(s32[1]{0:T(128)S(6)} %copy.14.count_ref, s32[64]{0:T(128)} %table_ref.1, s32[64]{0:T(128)} %bitcast.1, s32[64]{0:T(128)} %len_ref.1, s32[64,128]{1,0:T(8,128)} %rows_ref.1, s32[64,128]{1,0:T(8,128)} %slots_ref.1, bf16[20,2048,128]{2,1,0:T(8,128)(2,1)} %tables_ref.1), custom_call_target="tpu_custom_call" | custom-call | tf_op jit(solution)/shard_map/pool/pallas_call | solution.py:100
  21.6 76.9 %cross.1 = bf16[128,2560]{1,0:T(8,128)(2,1)} custom-call(bf16[160,128,128]{2,1,0:T(8,128)(2,1)} %pool.1.partial_ref, bf16[4,640,256]{2,1,0:T(8,128)(2,1)} %in_ref.1, bf16[4,256,256]{2,1,0:T(8,128)(2,1)} %mix_ref.1, bf16[4,256,640]{2,1,0:T(8,128)(2,1)} %out_w_ref.1, f32[4,2560]{1,0:T(4,128)} %bias_ref.1, bf16[4,2560]{1,0:T(4,128)(2,1)} %gate_ref.1), custom_call_target="tpu_custom_call" | custom-call | tf_op jit(solution)/shard_map/cross/pallas_call | solution.py:318
  98.5 2.0 %copy.15 = bf16[128,2560]{1,0:T(8,128)(2,1)} copy(bf16[128,2560]{1,0:T(8,128)(2,1)} %cross.1) | data formatting | bytes 1310720

commit v2 on v1

--- a/solution.py
+++ b/solution.py
@@ -11,27 +11,60 @@
 UNROLL = 4
 STREAMS = 4
 MESH = pl.DeviceIdType.MESH
+POOL_LIMIT = 30 << 20
+CROSS_LIMIT = 34 << 20
 VMEM_LIMIT = 67043328
 
 
 def pool_kernel(
     unroll,
     count_ref,
+    table_hbm,
+    peer_hbm,
+    len_hbm,
+    rows_hbm,
+    slots_hbm,
+    tables_hbm,
+    out_ref,
     table_ref,
     peer_ref,
     len_ref,
     rows_ref,
     slots_ref,
     tables_ref,
-    out_ref,
     acc,
     slot_of,
     key_of,
+    ready,
+    small_sem,
+    table_sem,
 ):
     table_count, rows_dev, width = tables_ref.shape
     total_blocks, block = rows_ref.shape
     tiles, samples, _ = out_ref.shape
-    count = count_ref[0]
+    pairs = (
+        (table_hbm, table_ref),
+        (peer_hbm, peer_ref),
+        (len_hbm, len_ref),
+        (rows_hbm, rows_ref),
+        (slots_hbm, slots_ref),
+    )
+    small = [pltpu.make_async_copy(a, b, small_sem.at[i]) for i, (a, b) in enumerate(pairs)]
+    for copy in small:
+        copy.start()
+
+    def table_copy(t):
+        return pltpu.make_async_copy(tables_hbm.at[t], tables_ref.at[t], table_sem.at[t])
+
+    for t in range(table_count):
+        table_copy(t).start()
+        ready[t] = 0
+
+    def need(t):
+        @pl.when(ready[t] == 0)
+        def _():
+            table_copy(t).wait()
+            ready[t] = 1
 
     def clear(i, carry):
         out_ref[i] = jnp.zeros((samples, width), jnp.bfloat16)
@@ -39,6 +72,9 @@
         return carry
 
     lax.fori_loop(0, tiles, clear, 0)
+    for copy in small:
+        copy.wait()
+    count = count_ref[0]
 
     lane = lax.broadcasted_iota(jnp.int32, (block, 128), 1)
     sample = lax.broadcasted_iota(jnp.int32, (samples, block), 0)
@@ -46,6 +82,8 @@
 
     def group(g, used):
         made = []
+        for u in range(unroll):
+            need(table_ref[g * unroll + u])
         for u in range(unroll):
             b = g * unroll + u
             row = rows_ref[pl.ds(b, 1), :]
@@ -88,6 +126,8 @@
         return carry
 
     lax.fori_loop(0, used, flush, 0)
+    for t in range(table_count):
+        need(t)
 
 
 def pool(peers, tables, block_rows, block_slots, block_table, block_peer, block_len, block_count):
@@ -95,21 +135,50 @@
     total_blocks = block_rows.shape[0]
     tiles = peers * table_count
     unroll = UNROLL if total_blocks % UNROLL == 0 else 1
-    smem = pl.BlockSpec(memory_space=pltpu.SMEM)
+    hbm = pl.BlockSpec(memory_space=pltpu.HBM)
     vmem = pl.BlockSpec(memory_space=pltpu.VMEM)
     return pl.pallas_call(
         functools.partial(pool_kernel, unroll),
         out_shape=jax.ShapeDtypeStruct((tiles, B_DEV, width), jnp.bfloat16),
-        in_specs=[smem] * 4 + [vmem] * 3,
+        in_specs=[pl.BlockSpec(memory_space=pltpu.SMEM)] + [hbm] * 6,
         out_specs=vmem,
         scratch_shapes=[
+            pltpu.SMEM((total_blocks,), jnp.int32),
+            pltpu.SMEM((total_blocks,), jnp.int32),
+            pltpu.SMEM((total_blocks,), jnp.int32),
+            pltpu.VMEM(block_rows.shape, jnp.int32),
+            pltpu.VMEM(block_slots.shape, jnp.int32),
+            pltpu.VMEM(tables.shape, jnp.bfloat16),
             pltpu.VMEM((total_blocks + 1, B_DEV, width), jnp.float32),
             pltpu.SMEM((tiles,), jnp.int32),
             pltpu.SMEM((total_blocks + 1,), jnp.int32),
+            pltpu.SMEM((table_count,), jnp.int32),
+            pltpu.SemaphoreType.DMA((5,)),
+            pltpu.SemaphoreType.DMA((table_count,)),
         ],
-        compiler_params=pltpu.CompilerParams(vmem_limit_bytes=VMEM_LIMIT),
+        compiler_params=pltpu.CompilerParams(
+            vmem_limit_bytes=POOL_LIMIT if peers <= 8 else VMEM_LIMIT
+        ),
+        cost_estimate=pl.CostEstimate(
+            flops=2 * total_blocks * B_DEV * tables.shape[1] * width,
+            bytes_accessed=2 * tables.size + 2 * tiles * B_DEV * width,
+            transcendentals=0,
+        ),
         name="pool",
-    )(block_count, block_table, block_peer[:, 0], block_len, block_rows, block_slots, tables)
+    )(
+        block_count,
+        *(
+            pltpu.with_memory_space_constraint(x, pltpu.HBM)
+            for x in (
+                block_table,
+                block_peer[:, 0],
+                block_len,
+                block_rows,
+                block_slots,
+                tables,
+            )
+        )
+    )
 
 
 def cross_kernel(
@@ -117,6 +186,7 @@
     share,
     partial_ref,
     in_ref,
+    far_ref,
     mix_ref,
     out_w_ref,
     bias_ref,
@@ -191,7 +261,7 @@
                 target = twin
             else:
                 _, place = piece_refs(q, across)
-                source = place
+                source = far_ref.at[q] if q < experts else place
                 target = twin
             return pltpu.make_async_remote_copy(
                 src_ref=source,
@@ -203,13 +273,20 @@
             )
 
         pieces = 2 * experts
-        for kind in (0, 1):
-            for q in range(pieces):
-                w_copy(kind, q).start()
+        for q in range(experts, pieces):
+            w_copy(0, q).start()
+        for q in range(experts):
+            w_copy(2, q).start()
+        for q in range(pieces):
+            w_copy(1, q).start()
         local = []
         for q in range(pieces):
             source, place = piece_refs(q, d)
             local.append(pltpu.make_async_copy(source, place, w_local.at[q]))
+            local[-1].start()
+        for q in range(experts):
+            _, place = piece_refs(q, across)
+            local.append(pltpu.make_async_copy(far_ref.at[q], place, w_local.at[pieces + q]))
             local[-1].start()
 
     def hop(step, last):
@@ -227,7 +304,7 @@
                 ring_copy(stream, held.at[step, stream], step + 1).start()
 
     if share:
-        passed = 0
+        passed = experts
         for step in range(peers - 2):
             hop(step, False)
             if 1 <= step and passed < pieces:
@@ -238,8 +315,8 @@
         for q in range(passed, pieces):
             w_copy(0, q).wait_recv()
             w_copy(2, q).start()
-        for q in range(pieces):
-            local[q].wait()
+        for copy in local:
+            copy.wait()
     else:
 
         def turn(step, carry):
@@ -299,15 +376,19 @@
     lax.fori_loop(1, peers - 1, sent, 0)
     if share:
         for kind in (0, 1, 2):
-            for q in range(pieces):
+            for q in range(experts if kind == 0 else 0, pieces):
                 w_copy(kind, q).wait_send()
 
 
-def cross(peers, groups, partial, cross_in, cross_mix, cross_out, cross_bias, gate_weight):
+def shared(peers, groups, cross_out):
+    return groups == 4 and cross_out.shape[2] % 128 == 0 and peers <= 8
+
+
+def cross(peers, groups, partial, cross_in, far_in, cross_mix, cross_out, cross_bias, gate_weight):
     tiles, samples, width = partial.shape
     table_count = tiles // peers
     experts = cross_in.shape[0]
-    share = groups == 4 and cross_out.shape[2] % 128 == 0 and peers <= 8
+    share = shared(peers, groups, cross_out)
     if not share:
         cross_in = lax.all_gather(cross_in, "dp", axis=1, tiled=True)
         cross_out = lax.all_gather(cross_out, "dp", axis=2, tiled=True)
@@ -318,7 +399,7 @@
     return pl.pallas_call(
         functools.partial(cross_kernel, peers, share),
         out_shape=jax.ShapeDtypeStruct((samples, table_count * width), jnp.bfloat16),
-        in_specs=[vmem] * 6,
+        in_specs=[vmem] * 7,
         out_specs=vmem,
         scratch_shapes=[
             pltpu.VMEM((peers - 1, STREAMS, table_count // STREAMS, samples, width), jnp.bfloat16),
@@ -329,13 +410,15 @@
             pltpu.SemaphoreType.DMA((STREAMS, peers - 1)),
             pltpu.SemaphoreType.DMA((3, 2 * experts)),
             pltpu.SemaphoreType.DMA((3, 2 * experts)),
-            pltpu.SemaphoreType.DMA((2 * experts,)),
+            pltpu.SemaphoreType.DMA((3 * experts,)),
         ],
         compiler_params=pltpu.CompilerParams(
-            collective_id=0, has_side_effects=True, vmem_limit_bytes=VMEM_LIMIT
+            collective_id=0,
+            has_side_effects=True,
+            vmem_limit_bytes=CROSS_LIMIT if peers <= 8 else VMEM_LIMIT,
         ),
         name="cross",
-    )(partial, cross_in, cross_mix, cross_out, cross_bias, gate_weight)
+    )(partial, cross_in, far_in, cross_mix, cross_out, cross_bias, gate_weight)
 
 
 def on_device(
@@ -353,10 +436,16 @@
     gate_weight,
 ):
     peers, groups = lax.axis_size("mp"), lax.axis_size("dp")
+    if shared(peers, groups, cross_out):
+        far_in = lax.ppermute(cross_in, "dp", [(i, (i + 2) % groups) for i in range(groups)])
+    else:
+        far_in = jnp.zeros((1, 8, 128), jnp.bfloat16)
     partial = pool(
         peers, tables, block_rows, block_slots, block_table, block_peer, block_len, block_count
     )
-    return cross(peers, groups, partial, cross_in, cross_mix, cross_out, cross_bias, gate_weight)
+    return cross(
+        peers, groups, partial, cross_in, far_in, cross_mix, cross_out, cross_bias, gate_weight
+    )
 
 
 def solution(mesh):

time: 101 us -> 91 us (0.901)
  the two profiles are of different devices: /device:TPU:25 before, /device:TPU:0 now
where the time goes in v2:
time: 91 us; the launch traced here: 90.8 us
  Pallas kernels  66.4 us (73%)
  waiting for transfers between devices  19.9 us (22%)
  starting transfers between devices  3 us (3%)
    pallas_call x1, Pallas kernels, cross(): pl.pallas_call(functools.partial(cross_kernel, peers, share), out_shape=j...  58 us
    ppermute x1, waiting for transfers between devices, on_device(): lax.ppermute(cross_in, 'dp', [(i, (i + 2) % groups) for i in range(groups)])  19.9 us
    pallas_call x1, Pallas kernels, pool(): pl.pallas_call(functools.partial(pool_kernel, unroll), out_shape=jax.Shap...  8.4 us
    ppermute x1, starting transfers between devices, on_device(): lax.ppermute(cross_in, 'dp', [(i, (i + 2) % groups) for i in range(groups)])  3 us
  transfers between devices with their start and end apart: 1, of which 1 were waited for; matrix products, arithmetic and copies ran while one was open for 0% of the time, Pallas kernels for 9%

profile of v2, /device:TPU:0, one launch (start us, length us, event | category | flops | bytes accessed | tf_op | source)
XLA Modules:
  0.0 90.8 jit_solution(2430959557313858968)
XLA Ops:
  0.0 3.0 %collective-permute-start = (bf16[4,640,256]{2,1,0:T(8,128)(2,1)}, bf16[4,640,256]{2,1,0:T(8,128)(2,1)S(1)}, u32[]{:S(2)}, u32[]{:S(2)}) collective-permute-start(bf16[4,640,256]{2,1,0:T(8,128)(2,1)} %in_ref.1), channel_id=1, source_target_pairs={{0,2},{1,3},{2,0},{3,1},{4,6},{5,7},{6,4},{7,5},{8,10},{9,11},{10,... | collective-permute-start | bytes 3932168 | tf_op jit(solution)/shard_map/ppermute | solution.py:440
  3.6 0.0 copy-start
  3.7 0.0 copy-start.1
  3.7 0.0 copy-start.2
  3.7 0.0 copy-start.3
  3.7 0.0 copy-start.4
  3.7 8.4 %pool.1.partial_ref = bf16[160,128,128]{2,1,0:T(8,128)(2,1)S(1)} custom-call(s32[1]{0:T(128)S(6)} %copy.14.count_ref, s32[64]{0:T(128)} %table_hbm.1, s32[64]{0:T(128)} %bitcast.1, s32[64]{0:T(128)} %len_hbm.1, s32[64,128]{1,0:T(8,128)} %rows_hbm.1, s32[64,128]{1,0:T(8,128)} %slots_hbm.1, bf16[20,2048,128]{2,1,0:T(8,128)(2,1)} %tables_hbm.1), custom_call_target="tpu_custom_call" | custom-call | flops 4294967296 | bytes 15728640 | tf_op jit(solution)/shard_map/pool/pallas_call | solution.py:140
  12.1 19.9 %collective-permute-done.far_ref = bf16[4,640,256]{2,1,0:T(8,128)(2,1)S(1)} collective-permute-done((bf16[4,640,256]{2,1,0:T(8,128)(2,1)}, bf16[4,640,256]{2,1,0:T(8,128)(2,1)S(1)}, u32[]{:S(2)}, u32[]{:S(2)}) %collective-permute-start) | collective-permute-done | bytes 1310752 | tf_op jit(solution)/shard_map/ppermute | solution.py:440
  32.0 0.0 copy-done
  32.0 0.0 copy-done.1
  32.0 0.0 copy-done.2
  32.0 0.0 copy-done.3
  32.0 0.0 copy-done.4
  32.0 58.0 %cross.1 = bf16[128,2560]{1,0:T(8,128)(2,1)S(1)} custom-call(bf16[160,128,128]{2,1,0:T(8,128)(2,1)S(1)} %pool.1.partial_ref, bf16[4,640,256]{2,1,0:T(8,128)(2,1)S(1)} %copy-done, bf16[4,640,256]{2,1,0:T(8,128)(2,1)S(1)} %collective-permute-done.far_ref, bf16[4,256,256]{2,1,0:T(8,128)(2,1)S(1)} %copy-done.2, bf16[4,256,640]{2,1,0:T(8,128)(2,1)S(1)} %copy-done.1, ...), custom_call_target="tpu_custom_call" | custom-call | tf_op jit(solution)/shard_map/cross/pallas_call | solution.py:399
  90.0 0.8 copy.15
Async XLA Ops:
  0.0 32.0 %collective-permute-start = (bf16[4,640,256]{2,1,0:T(8,128)(2,1)}, bf16[4,640,256]{2,1,0:T(8,128)(2,1)S(1)}, u32[]{:S(2)}, u32[]{:S(2)}) collective-permute-start(bf16[4,640,256]{2,1,0:T(8,128)(2,1)} %in_ref.1), channel_id=1, source_target_pairs={{0,2},{1,3},{2,0},{3,1},{4,6},{5,7},{6,4},{7,5},{8,10},{9,11},{10,... | collective-permute-start | bytes 3932168 | tf_op jit(solution)/shard_map/ppermute | solution.py:440
  3.6 28.3 %copy-start = (bf16[4,640,256]{2,1,0:T(8,128)(2,1)S(1)}, bf16[4,640,256]{2,1,0:T(8,128)(2,1)}, u32[]{:S(2)}) copy-start(bf16[4,640,256]{2,1,0:T(8,128)(2,1)} %in_ref.1) | copy-start | bytes 3932164
  3.7 28.3 %copy-start.1 = (bf16[4,256,640]{2,1,0:T(8,128)(2,1)S(1)}, bf16[4,256,640]{2,1,0:T(8,128)(2,1)}, u32[]{:S(2)}) copy-start(bf16[4,256,640]{2,1,0:T(8,128)(2,1)} %out_w_ref.1) | copy-start | bytes 3932164
  3.7 28.3 %copy-start.2 = (bf16[4,256,256]{2,1,0:T(8,128)(2,1)S(1)}, bf16[4,256,256]{2,1,0:T(8,128)(2,1)}, u32[]{:S(2)}) copy-start(bf16[4,256,256]{2,1,0:T(8,128)(2,1)} %mix_ref.1) | copy-start | bytes 1572868
  3.7 28.3 %copy-start.3 = (f32[4,2560]{1,0:T(4,128)S(1)}, f32[4,2560]{1,0:T(4,128)}, u32[]{:S(2)}) copy-start(f32[4,2560]{1,0:T(4,128)} %bias_ref.1) | copy-start | bytes 122884
  3.7 28.3 %copy-start.4 = (bf16[4,2560]{1,0:T(4,128)(2,1)S(1)}, bf16[4,2560]{1,0:T(4,128)(2,1)}, u32[]{:S(2)}) copy-start(bf16[4,2560]{1,0:T(4,128)(2,1)} %gate_ref.1) | copy-start | bytes 61444

commit v3 on v2

--- a/solution.py
+++ b/solution.py
@@ -8,7 +8,7 @@
 from jax.sharding import PartitionSpec as P
 
 B_DEV = 128
-UNROLL = 4
+UNROLL = 8
 STREAMS = 4
 MESH = pl.DeviceIdType.MESH
 POOL_LIMIT = 30 << 20
@@ -206,6 +206,7 @@
     table_count = tiles // peers
     part = table_count // STREAMS
     experts = mix_ref.shape[0]
+    ahead_count = far_ref.shape[0]
     me = lax.axis_index("mp")
     half = peers // 2
     at = jnp.where(lax.rem(me, 2) == 0, lax.div(me, 2), peers - 1 - lax.div(me, 2))
@@ -261,7 +262,7 @@
                 target = twin
             else:
                 _, place = piece_refs(q, across)
-                source = far_ref.at[q] if q < experts else place
+                source = far_ref.at[q] if q < ahead_count else place
                 target = twin
             return pltpu.make_async_remote_copy(
                 src_ref=source,
@@ -273,9 +274,9 @@
             )
 
         pieces = 2 * experts
-        for q in range(experts, pieces):
+        for q in range(ahead_count, pieces):
             w_copy(0, q).start()
-        for q in range(experts):
+        for q in range(ahead_count):
             w_copy(2, q).start()
         for q in range(pieces):
             w_copy(1, q).start()
@@ -284,7 +285,7 @@
             source, place = piece_refs(q, d)
             local.append(pltpu.make_async_copy(source, place, w_local.at[q]))
             local[-1].start()
-        for q in range(experts):
+        for q in range(ahead_count):
             _, place = piece_refs(q, across)
             local.append(pltpu.make_async_copy(far_ref.at[q], place, w_local.at[pieces + q]))
             local[-1].start()
@@ -304,7 +305,7 @@
                 ring_copy(stream, held.at[step, stream], step + 1).start()
 
     if share:
-        passed = experts
+        passed = ahead_count
         for step in range(peers - 2):
             hop(step, False)
             if 1 <= step and passed < pieces:
@@ -376,7 +377,7 @@
     lax.fori_loop(1, peers - 1, sent, 0)
     if share:
         for kind in (0, 1, 2):
-            for q in range(experts if kind == 0 else 0, pieces):
+            for q in range(ahead_count if kind == 0 else 0, pieces):
                 w_copy(kind, q).wait_send()
 
 
@@ -437,7 +438,7 @@
 ):
     peers, groups = lax.axis_size("mp"), lax.axis_size("dp")
     if shared(peers, groups, cross_out):
-        far_in = lax.ppermute(cross_in, "dp", [(i, (i + 2) % groups) for i in range(groups)])
+        far_in = lax.ppermute(cross_in[: cross_in.shape[0] - 1], "dp", [(i, (i + 2) % groups) for i in range(groups)])
     else:
         far_in = jnp.zeros((1, 8, 128), jnp.bfloat16)
     partial = pool(

time: 91 us -> 87.5 us (0.962)
  waiting for transfers between devices: 19.9 us -> 11.9 us
  Pallas kernels: 66.4 us -> 69.7 us
  local copies, waits for them, and re-layouts: 0.86 us -> 2.14 us
    ppermute x1, waiting for transfers between devices: 19.9 us -> 11.9 us  [on_device(): lax.ppermute(cross_in[:cross_in.shape[0] - 1], 'dp', [(i, (i + 2) % group...]
    pallas_call x1, Pallas kernels: 58 us -> 60.6 us  [cross(): pl.pallas_call(functools.partial(cross_kernel, peers, share), out_shape=j...]
    slice x0 -> x1, local copies, waits for them, and re-layouts: none -> 1.26 us  [on_device(): cross_in[:cross_in.shape[0] - 1]]
  transfers between devices with their start and end apart: 1 -> 1, of which waited for: 1 -> 1; matrix products, arithmetic and copies ran while one was open for 0% -> 0% of each run, Pallas kernels for 9% -> 10%
where the time goes in v3:
time: 87.5 us
  Pallas kernels  69.7 us (80%)
  waiting for transfers between devices  11.9 us (14%)
  starting transfers between devices  3.06 us (3%)
  local copies, waits for them, and re-layouts  2.14 us (2%)
    pallas_call x1, Pallas kernels, cross(): pl.pallas_call(functools.partial(cross_kernel, peers, share), out_shape=j...  60.6 us
    ppermute x1, waiting for transfers between devices, on_device(): lax.ppermute(cross_in[:cross_in.shape[0] - 1], 'dp', [(i, (i + 2) % group...  11.9 us
    pallas_call x1, Pallas kernels, pool(): pl.pallas_call(functools.partial(pool_kernel, unroll), out_shape=jax.Shap...  9.16 us
    ppermute x1, starting transfers between devices, on_device(): lax.ppermute(cross_in[:cross_in.shape[0] - 1], 'dp', [(i, (i + 2) % group...  3.06 us
  transfers between devices with their start and end apart: 1, of which 1 were waited for; matrix products, arithmetic and copies ran while one was open for 0% of the time, Pallas kernels for 10%

profile of v3, /device:TPU:0, one launch (start us, length us, event | category | flops | bytes accessed | tf_op | source)
XLA Modules:
  0.0 87.5 jit_solution(2900505364345377632)
XLA Ops:
  0.0 1.3 %slice.3 = bf16[3,640,256]{2,1,0:T(8,128)(2,1)S(1)} slice(bf16[4,640,256]{2,1,0:T(8,128)(2,1)} %in_ref.1), slice={[0:3], [0:640], [0:256]} | slice | bytes 1966080 | tf_op jit(solution)/shard_map/slice | solution.py:441
  1.3 3.1 %collective-permute-start = (bf16[3,640,256]{2,1,0:T(8,128)(2,1)S(1)}, bf16[3,640,256]{2,1,0:T(8,128)(2,1)S(1)}, u32[]{:S(2)}, u32[]{:S(2)}) collective-permute-start(bf16[3,640,256]{2,1,0:T(8,128)(2,1)S(1)} %slice.3), channel_id=1, source_target_pairs={{0,2},{1,3},{2,0},{3,1},{4,6},{5,7},{6,4},{7,5},{8,10},{9,11},{10,... | collective-permute-start | bytes 2949128 | tf_op jit(solution)/shard_map/ppermute | solution.py:441
  5.0 0.0 copy-start
  5.0 0.0 copy-start.1
  5.0 0.0 copy-start.2
  5.0 0.0 copy-start.3
  5.0 0.0 copy-start.4
  5.0 9.2 %pool.1.partial_ref = bf16[160,128,128]{2,1,0:T(8,128)(2,1)S(1)} custom-call(s32[1]{0:T(128)S(6)} %copy.14.count_ref, s32[64]{0:T(128)} %table_hbm.1, s32[64]{0:T(128)} %bitcast.1, s32[64]{0:T(128)} %len_hbm.1, s32[64,128]{1,0:T(8,128)} %rows_hbm.1, s32[64,128]{1,0:T(8,128)} %slots_hbm.1, bf16[20,2048,128]{2,1,0:T(8,128)(2,1)} %tables_hbm.1), custom_call_target="tpu_custom_call" | custom-call | flops 4294967296 | bytes 15728640 | tf_op jit(solution)/shard_map/pool/pallas_call | solution.py:140
  14.2 11.9 %collective-permute-done.far_ref = bf16[3,640,256]{2,1,0:T(8,128)(2,1)S(1)} collective-permute-done((bf16[3,640,256]{2,1,0:T(8,128)(2,1)S(1)}, bf16[3,640,256]{2,1,0:T(8,128)(2,1)S(1)}, u32[]{:S(2)}, u32[]{:S(2)}) %collective-permute-start) | collective-permute-done | bytes 983072 | tf_op jit(solution)/shard_map/ppermute | solution.py:441
  26.1 0.0 copy-done
  26.1 0.0 copy-done.1
  26.1 0.0 copy-done.2
  26.1 0.0 copy-done.3
  26.1 0.0 copy-done.4
  26.1 60.6 %cross.1 = bf16[128,2560]{1,0:T(8,128)(2,1)S(1)} custom-call(bf16[160,128,128]{2,1,0:T(8,128)(2,1)S(1)} %pool.1.partial_ref, bf16[4,640,256]{2,1,0:T(8,128)(2,1)S(1)} %copy-done, bf16[3,640,256]{2,1,0:T(8,128)(2,1)S(1)} %collective-permute-done.far_ref, bf16[4,256,256]{2,1,0:T(8,128)(2,1)S(1)} %copy-done.2, bf16[4,256,640]{2,1,0:T(8,128)(2,1)S(1)} %copy-done.1, ...), custom_call_target="tpu_custom_call" | custom-call | tf_op jit(solution)/shard_map/cross/pallas_call | solution.py:400
  86.7 0.8 copy.15
Async XLA Ops:
  1.3 24.8 %collective-permute-start = (bf16[3,640,256]{2,1,0:T(8,128)(2,1)S(1)}, bf16[3,640,256]{2,1,0:T(8,128)(2,1)S(1)}, u32[]{:S(2)}, u32[]{:S(2)}) collective-permute-start(bf16[3,640,256]{2,1,0:T(8,128)(2,1)S(1)} %slice.3), channel_id=1, source_target_pairs={{0,2},{1,3},{2,0},{3,1},{4,6},{5,7},{6,4},{7,5},{8,10},{9,11},{10,... | collective-permute-start | bytes 2949128 | tf_op jit(solution)/shard_map/ppermute | solution.py:441
  5.0 21.1 %copy-start = (bf16[4,640,256]{2,1,0:T(8,128)(2,1)S(1)}, bf16[4,640,256]{2,1,0:T(8,128)(2,1)}, u32[]{:S(2)}) copy-start(bf16[4,640,256]{2,1,0:T(8,128)(2,1)} %in_ref.1) | copy-start | bytes 3932164
  5.0 21.1 %copy-start.1 = (bf16[4,256,640]{2,1,0:T(8,128)(2,1)S(1)}, bf16[4,256,640]{2,1,0:T(8,128)(2,1)}, u32[]{:S(2)}) copy-start(bf16[4,256,640]{2,1,0:T(8,128)(2,1)} %out_w_ref.1) | copy-start | bytes 3932164
  5.0 21.1 %copy-start.2 = (bf16[4,256,256]{2,1,0:T(8,128)(2,1)S(1)}, bf16[4,256,256]{2,1,0:T(8,128)(2,1)}, u32[]{:S(2)}) copy-start(bf16[4,256,256]{2,1,0:T(8,128)(2,1)} %mix_ref.1) | copy-start | bytes 1572868
  5.0 21.1 %copy-start.3 = (f32[4,2560]{1,0:T(4,128)S(1)}, f32[4,2560]{1,0:T(4,128)}, u32[]{:S(2)}) copy-start(f32[4,2560]{1,0:T(4,128)} %bias_ref.1) | copy-start | bytes 122884
  5.0 21.1 %copy-start.4 = (bf16[4,2560]{1,0:T(4,128)(2,1)S(1)}, bf16[4,2560]{1,0:T(4,128)(2,1)}, u32[]{:S(2)}) copy-start(bf16[4,2560]{1,0:T(4,128)(2,1)} %gate_ref.1) | copy-start | bytes 61444
